TPU v7x, 256 devices: a whole 4x4x8 slice. The times are simulated.
256 devices in a mesh: ka: 64 (over x, z_hi, y), slab: 4 (over z_lo, core).
Axes of the slice: x: 4, y: 4, z: 8 (z_hi: 4, z_lo: 2; z = z_hi * 2 + z_lo), core: 2. Of those that a mesh axis runs over, the one named last changes fastest.
Arguments:
- val_wave: float32 [2, 64, 2, 12, 16, 128], P(None, 'ka', None, 'slab'), may hold values from -6 to 6
- cond_wave: float32 [2, 64, 8, 12, 16, 128], P(None, 'ka', None, 'slab'), may hold values from -6 to 6
- val_energy: float32 [64, 2], P('ka'), may hold values from -2 to -0.5
- cond_energy: float32 [64, 8], P('ka'), may hold values from 0.5 to 3
- frequency: float32 [4], replicated, may hold values from 0.2 to 4
- kpoint_map: int32 [64], replicated, may hold values from 0 to 63, as said below
- umklapp: int32 [3, 64], replicated, may hold values from 0 to 1, as said below
- gvector_index: int32 [6144], replicated, may hold values from 0 to 24575, as said below
Outputs:
- polarizability: float32 [4, 2, 6144, 6144], P(None, None, 'ka', 'slab')
Inputs may be any that keep to these rules, and one draw needn't show every extreme that they name: With s the integer for which s * s * s = 64 and k = s * s * i + s * j + l, kpoint_map[k] is the index of (i + q0, j + q1, l + q2) taken modulo s in each coordinate, for one vector q whose components lie in 0 to s - 1, not all zero. umklapp[d, k] is 1 where coordinate d of k plus component d of q reaches s, else 0. `gvector_index`: entries are distinct.
All inputs are finite; a program needn't handle non-finite values.
Results may differ from a plain program's by a relative error of at most 0.0038.
Values may be sent and summed in bfloat16 or wider, within the bound.
A program may use at most 128 MiB of HBM per device.

v0:
```python
import functools
import math

import jax
import jax.numpy as jnp
import numpy as np
from jax import lax
from jax.experimental import pallas as pl
from jax.experimental.pallas import tpu as pltpu
from jax.sharding import PartitionSpec as P

HIGH = lax.Precision.HIGHEST
MESH = pl.DeviceIdType.MESH
f32, bf16 = jnp.float32, jnp.bfloat16
TILE = 512
SIDE = 4
CUT = 384
EXTRA = 128
ORDER = (
    "S0", "C00", "C01", "C02", "rs1_0", "C03", "S1", "C10", "C11", "fin_0", "Hs00", "Hs01", "Is000",
    "Is010", "C12", "rs1_1", "C13", "Itm000", "Itp000", "Itm010", "Itp010", "Htm00", "Htp00",
    "Is001", "Is002", "Htm01", "Htp01", "Is011", "Is012", "Os000", "Os010", "fin_1", "Hs10", "Hs11",
    "Is100", "Is110", "Itm001", "Itp001", "Itm002", "Itp002", "Is003", "Itm011", "Itp011", "Itm012",
    "Itp012", "Is013", "Otm010", "Otp010", "Itm100", "Itp100", "Htm10", "Htp10", "Is101", "Is102",
    "Otm000", "Otp000", "Os001", "Os002", "Itm110", "Itp110", "Os011", "Itm003", "Itp003", "Htm11",
    "Htp11", "Is111", "Is112", "Os012", "Itp013", "Itm013", "Os100", "R00", "Is103", "Itm101",
    "Itp101", "Itm102", "Itp102", "Is113", "Otm001", "Otp001", "Otm011", "Otp011", "Os003", "M00",
    "Itm111", "Itp111", "Itm112", "Itp112", "Otm002", "Otp002", "Os110", "Os013", "Otm012",
    "Otp012", "Itm103", "Itp103", "Os101", "Os102", "Otp100", "Otm100", "Itp113", "Itm113", "R01",
    "Otm110", "Otp110", "Otp003", "Otm003", "Os111", "Os112", "Otm013", "Otp013", "M01", "Os103",
    "R02", "Otp101", "Otm101", "Otp102", "Otm102", "Otm111", "Otp111", "R10", "Os113", "M02",
    "Otm112", "Otp112", "R03", "Otp103", "Otm103", "M10", "Otm113", "Otp113", "R11", "M03", "R12",
    "R13", "M11", "M12", "M13",
)


def y_table(bands, extent):
    index = np.arange(extent)
    angle = 2 * np.pi * (np.outer(index, index) % extent) / extent
    eye = np.eye(bands)
    size = bands * extent
    cos = np.einsum("ky,cd->kcdy", np.cos(angle), eye).reshape(size, size)
    sin = np.einsum("ky,cd->kcdy", np.sin(angle), eye).reshape(size, size)
    return np.block([[cos, sin], [-sin, cos]]).astype(np.float32)


def z_table(extent):
    index = np.arange(extent)
    angle = 2 * np.pi * (np.outer(index, index) % extent) / extent
    cos, sin = np.cos(angle), np.sin(angle)
    return np.block([[cos, -sin], [sin, cos]]).astype(np.float32)


def x_table(extent, norm):
    index = np.arange(extent)
    angle = 2 * np.pi * (np.outer(index, index) % extent) / extent
    return (np.concatenate([np.cos(angle), np.sin(angle)], 1) * norm).astype(np.float32)


def split_rows(value):
    high = value.astype(bf16)
    return high, (value - high.astype(f32)).astype(bf16)


def split_table(table, axis):
    high = table.astype(jnp.bfloat16)
    low = (table - high.astype(np.float32)).astype(jnp.bfloat16)
    return jnp.asarray(np.concatenate([high, high, low], axis))


def kernel(
    kpoints, row_g, shift, xtab, freq, cond_e, packed, cond, gvec, ytab, ztab, out,
    g00, g01, g10, g11, part, r1, s2, r2, spec, phase, wtile, rt, left, sel, wsel,
    send, recv, rsend, rrecv,
):
    ka = lax.axis_index("ka")
    slab = lax.axis_index("slab")
    zlo, core = slab // 2, slab % 2
    block_g = part.shape[3]
    half_g = block_g // 2
    freqs = freq.shape[0]
    coords = (ka // (SIDE * SIDE), ka // SIDE % SIDE, ka % SIDE)
    xi, hi, yi = coords
    bands, planes, ny, nz = cond.shape[1:]
    nv = 2
    nx = xtab.shape[0]
    rows = bands * ny
    height = planes * 2 * bands
    fields = nv * 2 * planes
    bufs = ((g00, g01), (g10, g11))

    def neighbour(axis, move):
        if axis == "x":
            return ((xi + move) % SIDE * 16 + hi * 4 + yi, slab)
        if axis == "h":
            return (xi * 16 + (hi + move) % SIDE * 4 + yi, slab)
        return (xi * 16 + hi * 4 + (yi + move) % SIDE, slab)

    peers = [(ka, (slab + d) % 4) for d in range(1, 4)]
    partner = (ka, zlo * 2 + 1 - core)
    across = (ka, (1 - zlo) * 2 + core)

    barrier = pltpu.get_barrier_semaphore()
    friends = [neighbour(axis, move) for axis in "xhy" for move in (1, 3)] + peers
    for friend in friends:
        pl.semaphore_signal(barrier, inc=1, device_id=friend, device_id_type=MESH)

    copies, waited = {}, set()

    def start(name, src, dst, device):
        k = len(copies)
        c = pltpu.make_async_remote_copy(
            src_ref=src, dst_ref=dst, send_sem=send.at[k], recv_sem=recv.at[k],
            device_id=device, device_id_type=MESH,
        )
        copies[name] = c
        c.start()

    def need(*names):
        for name in names:
            if name not in waited:
                waited.add(name)
                copies[name].wait_recv()

    q = shift[0]
    folds = [
        (coords[d] < q // SIDE ** (2 - d) % SIDE).astype(jnp.int32) for d in range(3)
    ]
    targets = [
        (1 - zlo) * 2 + 1 - core,
        (1 - zlo) * 2 + core,
        zlo * 2 + 1 - core,
        zlo * 2 + core,
    ]

    owner = ka * row_g // block_g
    at = ka * row_g - owner * block_g
    side_q = at // half_g
    line = lax.broadcasted_iota(jnp.int32, sel.shape, 0)
    lane = lax.broadcasted_iota(jnp.int32, sel.shape, 1)
    sel[...] = (lane == line + at - side_q * half_g).astype(f32).astype(bf16)
    for v in range(nv):
        line = lax.broadcasted_iota(jnp.int32, wsel.shape[1:], 0)
        lane = lax.broadcasted_iota(jnp.int32, wsel.shape[1:], 1)
        wsel[v] = ((lane == line + 3 * freqs * v) & (line < 3 * freqs)).astype(f32).astype(bf16)

    def weights():
        shape = (2 * bands, EXTRA)
        lane = lax.broadcasted_iota(jnp.int32, shape, 1)
        row = lax.broadcasted_iota(jnp.int32, shape, 0)
        level = jnp.zeros(shape, f32)
        for c in range(bands):
            level = jnp.where((row == c) | (row == bands + c), cond_e[0, c], level)
        omega = jnp.ones(shape, f32)
        value = jnp.zeros(shape, f32)
        for v in range(nv):
            for w in range(freqs):
                first = 3 * (v * freqs + w)
                omega = jnp.where((lane >= first) & (lane < first + 3), freq[w], omega)
        for v in range(nv):
            gap = packed[fields, 0:1, v : v + 1] - level
            weight = 2.0 * gap / (gap * gap + omega * omega) / kpoints
            high = weight.astype(bf16).astype(f32)
            mid = (weight - high).astype(bf16).astype(f32)
            low = weight - high - mid
            piece = lane % 3
            pieces = jnp.where(piece == 0, high, jnp.where(piece == 1, mid, low))
            first = 3 * v * freqs
            value = jnp.where((lane >= first) & (lane < first + 3 * freqs), pieces, value)
        wtile[...] = value.astype(bf16)

    def spectrum(v):
        columns = []
        for x in range(planes):
            vr = packed[v * planes + x][None]
            vi = packed[(nv + v) * planes + x][None]
            cr, ci = cond[0, :, x], cond[1, :, x]
            re = (vr * cr + vi * ci).reshape(rows, nz)
            im = (vr * ci - vi * cr).reshape(rows, nz)
            columns.append(jnp.concatenate([re, im], 0))
        high, low = split_rows(jnp.concatenate(columns, 1))
        t = jnp.dot(ytab[...], jnp.concatenate([high, low, high], 0), preferred_element_type=f32)
        t = [
            jnp.concatenate([t[:rows, x * nz : (x + 1) * nz], t[rows:, x * nz : (x + 1) * nz]], 1)
            for x in range(planes)
        ]
        high, low = split_rows(jnp.concatenate(t, 0))
        f = jnp.dot(jnp.concatenate([high, low, high], 1), ztab[...], preferred_element_type=f32)
        for x in range(planes):
            fx = f[x * rows : (x + 1) * rows]
            both = [fx[:, :nz].reshape(ny, bands, nz), fx[:, nz:].reshape(ny, bands, nz)]
            both = jnp.concatenate(both, 1).reshape(ny // 2, 2, 2 * bands, nz)
            for odd in range(2):
                high, low = split_rows(both[:, odd])
                here = slice(2 * bands * x, 2 * bands * (x + 1))
                spec[:, here, odd * nz : (odd + 1) * nz] = high
                spec[:, here, (2 + odd) * nz : (3 + odd) * nz] = low

    def columns_of(v, j):
        def step(i, _):
            cols = pl.ds(pl.multiple_of(targets[j] * block_g + i * TILE, TILE), TILE)
            local = pl.ds(pl.multiple_of(i * TILE, TILE), TILE)
            g = gvec[:, cols]
            gz = (g % nz - folds[2] + nz) % nz
            gy = (g // nz % ny - folds[1] + ny) % ny
            if v == 0:
                gx = g // (nz * ny) - folds[0]
                gx = jnp.where(gx < 0, gx + nx, gx)
                cosines = [jnp.zeros((1, TILE), f32) for _ in range(planes)]
                sines = list(cosines)
                for m in range(nx):
                    same = gx == m
                    for x in range(planes):
                        plane = slab * planes + x
                        cosines[x] = jnp.where(same, xtab[plane, m], cosines[x])
                        sines[x] = jnp.where(same, xtab[plane, nx + m], sines[x])
                for x in range(planes):
                    phase[x : x + 1, cols] = cosines[x]
                    phase[planes + x : planes + x + 1, cols] = sines[x]
            else:
                cosines = [phase[x : x + 1, cols] for x in range(planes)]
                sines = [phase[planes + x : planes + x + 1, cols] for x in range(planes)]
            code = gz + gy % 2 * nz
            hot = (lax.broadcasted_iota(jnp.int32, (2 * nz, TILE), 0) == code).astype(f32).astype(bf16)
            hot = jnp.concatenate([hot, hot], 0)
            table = spec[...].reshape(ny // 2 * height, 4 * nz)
            picked = jnp.dot(table, hot, preferred_element_type=f32)
            which = jnp.broadcast_to(gy // 2, (height, TILE))
            acc = picked[:height]
            for k in range(1, ny // 2):
                acc = jnp.where(which == k, picked[k * height : (k + 1) * height], acc)
            re, im = 0.0, 0.0
            for x in range(planes):
                a = x * 2 * bands
                sre, sim = acc[a : a + bands], acc[a + bands : a + 2 * bands]
                re = re + (sre * cosines[x] + sim * sines[x])
                im = im + (sim * cosines[x] - sre * sines[x])
            part[v, j, :, local] = jnp.concatenate([re, im], 0)
            return 0

        lax.fori_loop(0, block_g // TILE, step, 0)

    actions = {}

    def add(name, call):
        actions[name] = call

    def first_columns():
        columns_of(0, 0)
        pl.semaphore_wait(barrier, len(friends))
        start("ra0", part.at[0, 0], r1.at[0, 0], partner)

    def compute(v, j):
        if (v, j) == (0, 0):
            return first_columns
        if j % 2:
            return lambda: columns_of(v, j)

        def call():
            columns_of(v, j)
            name = ("ra", None, "rb")[j] + str(v)
            start(name, part.at[v, j], r1.at[v, j // 2], partner)

        return call

    def across_sum(v):
        def call():
            need(f"ra{v}")
            s2[v] = part[v, 1] + r1[v, 0]
            start(f"r2{v}", s2.at[v], r2.at[v], across)

        return call

    def finish_block(v):
        def call():
            need(f"rb{v}", f"r2{v}")
            total = (part[v, 3] + r1[v, 1] + r2[v]).astype(bf16)
            bufs[v][0][0, 0, 0] = total[:, :half_g]
            if v == 0:
                bufs[v][1][0, 0, 0, :, :half_g] = total[:, half_g:]
                bufs[v][1][0, 0, 0, :, half_g:] = wtile[...]
            else:
                bufs[v][1][0, 0, 0] = total[:, half_g:]

        return call

    def ring(one, two, names, axis, slots, low, high):
        def begin():
            start(one + "p", slots(0), slots(1), neighbour(axis, 1))
            start(one + "m", slots(0), slots(2), neighbour(axis, 3))

        def forward():
            need(one + "p")
            start(two + "p", low(slots(1)), low(slots(3)), neighbour(axis, 1))

        def back():
            need(one + "m")
            start(two + "m", high(slots(2)), high(slots(3)), neighbour(axis, 3))

        for name, call in zip(names, (begin, forward, back)):
            add(name, call)

    def after(events, name):
        inner_call = actions[name]

        def call():
            need(*events)
            inner_call()

        actions[name] = call

    def low_lanes(ref):
        return ref.at[:, pl.ds(0, CUT)]

    def high_lanes(ref):
        return ref.at[:, pl.ds(CUT, ref.shape[1] - CUT)]

    def low_blocks(ref):
        return ref.at[pl.ds(0, 2)]

    def high_blocks(ref):
        return ref.at[pl.ds(2, 2)]

    row_copies = {}

    def natural(v, side, h, cols):
        g = bufs[v][side]
        if side:
            return g[h, :, :, :, cols].reshape(SIDE * SIDE * 2 * bands, -1)
        return jnp.concatenate([g[h, y, x, :, cols] for x in range(SIDE) for y in range(SIDE)], 0)

    transposed = (((1,), (1,)), ((), ()))

    def ship_rows(v, h):
        chunk = v * SIDE + h

        def call():
            need(*[f"O{v}{side}{h}2{way}" for side in range(2) for way in "pm"])
            held = [
                pltpu.make_async_remote_copy(
                    src_ref=rt.at[chunk], dst_ref=rt.at[chunk], send_sem=rsend.at[chunk, d],
                    recv_sem=rrecv.at[chunk], device_id=peers[d], device_id_type=MESH,
                )
                for d in range(3)
            ]
            row_copies[chunk] = held

            @pl.when(slab == owner)
            def _():
                tiles = natural(0, 1, h, pl.ds(half_g, EXTRA))
                w = lax.dot_general(wsel[v], tiles, transposed, preferred_element_type=f32)
                rt[chunk, row_g:] = w.astype(bf16)
                for side in range(2):

                    @pl.when(side_q == side)
                    def _():
                        block = natural(v, side, h, pl.ds(0, half_g))
                        picked = lax.dot_general(sel[...], block, transposed, preferred_element_type=f32)
                        rt[chunk, :row_g] = picked.astype(bf16)

                for c in held:
                    c.start()

        return call

    def multiply(v, h):
        chunk = v * SIDE + h

        def call():
            @pl.when(slab != owner)
            def _():
                row_copies[chunk][0].wait_recv()

            both = rt[chunk].astype(f32)
            base = both[:row_g]
            spot = lax.broadcasted_iota(jnp.int32, base.shape, 1)
            swapped = jnp.where(spot % 16 < 8, pltpu.roll(base, 248, 1), -pltpu.roll(base, 8, 1))
            for w in range(freqs):
                k = row_g + 3 * w
                scale = both[k : k + 1] + both[k + 1 : k + 2] + both[k + 2 : k + 3]
                left[2 * w * row_g : (2 * w + 1) * row_g] = (base * scale).astype(bf16)
                left[(2 * w + 1) * row_g : (2 * w + 2) * row_g] = (swapped * scale).astype(bf16)
            for side in range(2):

                def column(i, _, side=side):
                    cols = pl.ds(pl.multiple_of(i * 256, 256), 256)
                    there = pl.ds(pl.multiple_of(side * half_g + i * 256, 256), 256)
                    product = jnp.dot(left[...], natural(v, side, h, cols), preferred_element_type=f32)
                    if chunk == 0:
                        out[:, there] = product
                    else:
                        out[:, there] += product
                    return 0

                lax.fori_loop(0, half_g // 256, column, 0)

        return call

    for v in range(nv):
        add(f"S{v}", lambda v=v: spectrum(v))
        for j in range(4):
            add(f"C{v}{j}", compute(v, j))
        add(f"rs1_{v}", across_sum(v))
        add(f"fin_{v}", finish_block(v))
        for side in range(2):
            g = bufs[v][side]
            k = f"{v}{side}"
            inner, outer = ("x", "y") if side == 0 else ("y", "x")
            ring(f"H{k}1", f"H{k}2", (f"Hs{k}", f"Htp{k}", f"Htm{k}"), "h",
                 lambda j, g=g: g.at[j, 0, 0], low_lanes, high_lanes)
            for h in range(SIDE):
                ring(f"I{k}{h}1", f"I{k}{h}2", (f"Is{k}{h}", f"Itp{k}{h}", f"Itm{k}{h}"), inner,
                     lambda j, g=g, h=h: g.at[h, 0, j], low_lanes, high_lanes)
                ring(f"O{k}{h}1", f"O{k}{h}2", (f"Os{k}{h}", f"Otp{k}{h}", f"Otm{k}{h}"), outer,
                     lambda j, g=g, h=h: g.at[h, j], low_blocks, high_blocks)
                before = ((), (f"H{k}1p",), (f"H{k}1m",), (f"H{k}2p", f"H{k}2m"))[h]
                after(before, f"Is{k}{h}")
                after([f"I{k}{h}{n}{way}" for n in "12" for way in "pm"], f"Os{k}{h}")
        for h in range(SIDE):
            add(f"R{v}{h}", ship_rows(v, h))
            add(f"M{v}{h}", multiply(v, h))

    weights()
    for name in ORDER:
        actions.pop(name)()
    assert not actions

    for c in copies.values():
        c.wait_send()

    @pl.when(slab == owner)
    def _():
        for held in row_copies.values():
            for c in held:
                c.wait_send()


def kernel_call(shift, freq, cond_e, packed, cond, gvec, norm, slabs, kpoints):
    bands, planes, ny, nz = cond.shape[1:]
    total = gvec.shape[1]
    nx = planes * slabs
    block_g, row_g, freqs = total // slabs, total // kpoints, freq.shape[0]
    half = 2 * bands
    tall = (row_g + 3 * freqs + 15) // 16 * 16
    vm = pl.BlockSpec(memory_space=pltpu.VMEM)
    sm = pl.BlockSpec(memory_space=pltpu.SMEM)
    count = 3 * 2 + 4 * (4 + 16 + 16)
    return pl.pallas_call(
        functools.partial(kernel, float(kpoints), row_g),
        out_shape=jax.ShapeDtypeStruct((freqs * 2 * row_g, block_g), f32),
        in_specs=[sm] * 4 + [vm] * 5,
        out_specs=vm,
        scratch_shapes=[
            pltpu.VMEM((4, 4, 4, half, block_g // 2), bf16),
            pltpu.VMEM((4, 4, 4, half, block_g // 2 + EXTRA), bf16),
            pltpu.VMEM((4, 4, 4, half, block_g // 2), bf16),
            pltpu.VMEM((4, 4, 4, half, block_g // 2), bf16),
            pltpu.VMEM((2, 4, half, block_g), f32),
            pltpu.VMEM((2, 2, half, block_g), f32),
            pltpu.VMEM((2, half, block_g), f32),
            pltpu.VMEM((2, half, block_g), f32),
            pltpu.VMEM((ny // 2, planes * half, 4 * nz), bf16),
            pltpu.VMEM((8, total), f32),
            pltpu.VMEM((half, EXTRA), bf16),
            pltpu.VMEM((8, tall, 256), bf16),
            pltpu.VMEM((freqs * 2 * row_g, 256), bf16),
            pltpu.VMEM((row_g, block_g // 2), bf16),
            pltpu.VMEM((2, tall - row_g, EXTRA), bf16),
            pltpu.SemaphoreType.DMA((count,)),
            pltpu.SemaphoreType.DMA((count,)),
            pltpu.SemaphoreType.DMA((8, 3)),
            pltpu.SemaphoreType.DMA((8,)),
        ],
        compiler_params=pltpu.CompilerParams(
            collective_id=0, has_side_effects=True, vmem_limit_bytes=48 * 1024 * 1024
        ),
        cost_estimate=pl.CostEstimate(flops=10**10, bytes_accessed=10**7, transcendentals=0),
        name="response",
    )(
        shift,
        jnp.asarray(x_table(nx, norm)),
        freq,
        cond_e,
        packed,
        cond,
        gvec,
        split_table(y_table(bands, ny), 1),
        split_table(z_table(nz), 0),
    )


def shifted_target(index, shift, side):
    target = 0
    for stride in (side * side, side, 1):
        target += (index // stride + shift // stride) % side * stride
    return target


def route(payload, shift, side):
    count = side**3

    def along(offset):
        pairs = [(i, shifted_target(i, offset, side)) for i in range(count)]
        return lambda block: lax.ppermute(block, "ka", pairs)

    middle = shift // side % side
    outer = shift // (side * side) * side + shift % side
    ends = [i // side * side * side + i % side for i in range(1, side * side)]
    payload = lax.switch(middle, [lambda block: block] + [along(i * side) for i in range(1, side)], payload)
    return lax.switch(outer, [lambda block: block] + [along(i) for i in ends], payload)


def per_device(
    val_wave, cond_wave, val_energy, cond_energy, frequency, kpoint_map, umklapp, gvector_index
):
    slab_count = lax.axis_size("slab")
    kpoint_count = lax.axis_size("ka")
    side = max((candidate for candidate in range(1, 9) if candidate**3 <= kpoint_count))
    shift = kpoint_map[0]
    planes, extent_y, extent_z = val_wave.shape[3:]
    fields = val_wave.shape[0] * val_wave.shape[2] * planes
    levels = jnp.pad(val_energy, ((0, extent_y - 1), (0, extent_z - val_energy.shape[1])))
    packed = jnp.concatenate([val_wave.reshape(fields, extent_y, extent_z), levels[None]], 0)
    packed = route(packed, shift, side)
    points = planes * slab_count * extent_y * extent_z
    norm = 1.0 / (2.0 * math.sqrt(points))
    freq_count = frequency.shape[0]
    total_g = gvector_index.shape[0]
    row_g = total_g // kpoint_count
    product = kernel_call(
        kpoint_map, frequency, cond_energy, packed, cond_wave[:, 0], gvector_index[None], norm,
        slab_count, kpoint_count,
    )
    return product.reshape(freq_count, 2, row_g, total_g // slab_count)


def solution(mesh):
    return jax.shard_map(
        per_device,
        mesh=mesh,
        in_specs=(
            P(None, "ka", None, "slab", None, None),
            P(None, "ka", None, "slab", None, None),
            P("ka", None),
            P("ka", None),
            P(),
            P(),
            P(),
            P(),
        ),
        out_specs=P(None, None, "ka", "slab"),
        check_vma=False,
    )
```

profile of v0, /device:TPU:33, one launch (start us, length us, event | category | flops | bytes accessed | tf_op | source)
XLA Modules:
  0.0 95.7 jit_solution(16227339237469659255)
XLA Ops:
  2.6 0.7 pad_bitcast_fusion
  3.3 0.9 pad_maximum_fusion
  4.2 10.4 %conditional.2 = (f32[13,16,128]{2,1,0:T(8,128)S(1)}) conditional(s32[]{:T(128)} %clamp.7, f32[13,16,128]{2,1,0:T(8,128)S(1)} %pad_maximum_fusion, f32[13,16,128]{2,1,0:T(8,128)S(1)} %pad_maximum_fusion, f32[13,16,128]{2,1,0:T(8,128)S(1)} %pad_maximum_fusion, f32[13,16,128]{2,1,0:T(8,128)S(1)} %pad_maximum_fusion), branch_computations={%region_0.1_spmd, %region_1.2_spmd, %region_2.3_spmd, %region_3.4_... | conditional | bytes 639024 | solution.py:509
  4.2 3.0 %collective-permute-start = (f32[13,16,128]{2,1,0:T(8,128)S(1)}, f32[13,16,128]{2,1,0:T(8,128)S(1)}, u32[]{:S(2)}, u32[]{:S(2)}) collective-permute-start(f32[13,16,128]{2,1,0:T(8,128)S(1)} %param.1), channel_id=1, source_target_pairs={{0,16},{4,20},{8,24},{12,28},{16,32},{20,36},{24,40},{28,44},{32,4... | collective-permute-start | bytes 319496 | tf_op jit(solution)/shard_map/cond/branch_1_fun/ppermute | solution.py:504
  7.2 7.4 %collective-permute-done = f32[13,16,128]{2,1,0:T(8,128)S(1)} collective-permute-done((f32[13,16,128]{2,1,0:T(8,128)S(1)}, f32[13,16,128]{2,1,0:T(8,128)S(1)}, u32[]{:S(2)}, u32[]{:S(2)}) %collective-permute-start) | collective-permute-done | bytes 106528 | tf_op jit(solution)/shard_map/cond/branch_1_fun/ppermute | solution.py:504
  14.6 5.4 %conditional.3 = (f32[13,16,128]{2,1,0:T(8,128)S(1)}) conditional(s32[]{:T(128)} %clamp.6, f32[13,16,128]{2,1,0:T(8,128)S(1)} %get-tuple-element.47, f32[13,16,128]{2,1,0:T(8,128)S(1)} %get-tuple-element.47, f32[13,16,128]{2,1,0:T(8,128)S(1)} %get-tuple-element.47, f32[13,16,128]{2,1,0:T(8,128)S(1)} %get-tuple-element.47, ...), branch_computations={%region_4.5_spmd, %region_5.6_spmd, %region_6.7_spmd, %region_7.8_... | conditional | bytes 639024 | solution.py:510
  14.7 3.0 %collective-permute-start.4 = (f32[13,16,128]{2,1,0:T(8,128)S(1)}, f32[13,16,128]{2,1,0:T(8,128)S(1)}, u32[]{:S(2)}, u32[]{:S(2)}) collective-permute-start(f32[13,16,128]{2,1,0:T(8,128)S(1)} %param.6), channel_id=1, source_target_pairs={{0,8},{4,12},{8,0},{12,4},{16,24},{20,28},{24,16},{28,20},{32,40},... | collective-permute-start | bytes 319496 | tf_op jit(solution)/shard_map/cond/branch_2_fun/ppermute | solution.py:504
  17.7 2.1 %collective-permute-done.4 = f32[13,16,128]{2,1,0:T(8,128)S(1)} collective-permute-done((f32[13,16,128]{2,1,0:T(8,128)S(1)}, f32[13,16,128]{2,1,0:T(8,128)S(1)}, u32[]{:S(2)}, u32[]{:S(2)}) %collective-permute-start.4) | collective-permute-done | bytes 106528 | tf_op jit(solution)/shard_map/cond/branch_2_fun/ppermute | solution.py:504
  20.0 0.0 copy-start
  20.0 0.6 copy-done
  20.7 0.0 copy-start.1
  20.7 1.0 %copy-done.1 = f32[2,1,8,3,16,128]{5,4,3,2,1,0:T(8,128)S(1)} copy-done((f32[2,1,8,3,16,128]{5,4,3,2,1,0:T(8,128)S(1)}, f32[2,1,8,3,16,128]{5,4,3,2,1,0:T(8,128)}, u32[]{:S(2)}) %copy-start.1) | copy-done | bytes 393240
  21.7 0.0 copy-start.2
  21.7 0.7 copy-done.2
  22.4 0.0 copy-start.3
  22.4 0.7 copy-done.3
  23.1 0.0 copy-start.4
  23.1 0.7 copy-done.4
  23.7 0.0 copy-start.5
  23.7 1.0 %copy-done.5 = bf16[768,256]{1,0:T(8,128)(2,1)S(1)} copy-done((bf16[768,256]{1,0:T(8,128)(2,1)S(1)}, bf16[768,256]{1,0:T(8,128)(2,1)}, u32[]{:S(2)}) %copy-start.5) | copy-done | bytes 393240
  24.7 1.0 %copy-done.6 = bf16[256,768]{1,0:T(8,128)(2,1)S(1)} copy-done((bf16[256,768]{1,0:T(8,128)(2,1)S(1)}, bf16[256,768]{1,0:T(8,128)(2,1)}, u32[]{:S(2)}) %copy-start.6) | copy-done | bytes 393240
  25.7 0.7 copy-done.7
  26.4 67.1 %response.1 = f32[768,1536]{1,0:T(8,128)S(1)} custom-call(s32[64]{0:T(128)S(1)} %copy-done, f32[12,24]{1,0:T(8,128)S(1)} %copy-done.7, f32[4]{0:T(128)S(1)} %copy-done.3, f32[1,8]{1,0:T(1,128)S(1)} %copy-done.4, f32[13,16,128]{2,1,0:T(8,128)S(1)} %get-tuple-element.48.packed, f32[2,8,3,16,128]{4,3,2,1,0:T(8,128)S(1)} %bitcast.13, s32[1,6144]{1,0:T(1,128)S(1)} %bitcast.14, ...), custom_call_target="tpu_custom_call" | custom-call | flops 10000000000 | bytes 10000000 | tf_op jit(solution)/shard_map/response/pallas_call | solution.py:448
  93.5 2.2 %copy.32 = f32[4,2,96,1536]{3,2,1,0:T(8,128)} copy(f32[4,2,96,1536]{3,2,1,0:T(8,128)S(1)} %bitcast.8) | data formatting | bytes 9437184
  (4 shorter events, 0.0 us)
Async XLA Ops:
  4.2 10.4 %collective-permute-start = (f32[13,16,128]{2,1,0:T(8,128)S(1)}, f32[13,16,128]{2,1,0:T(8,128)S(1)}, u32[]{:S(2)}, u32[]{:S(2)}) collective-permute-start(f32[13,16,128]{2,1,0:T(8,128)S(1)} %param.1), channel_id=1, source_target_pairs={{0,16},{4,20},{8,24},{12,28},{16,32},{20,36},{24,40},{28,44},{32,4... | collective-permute-start | bytes 319496 | tf_op jit(solution)/shard_map/cond/branch_1_fun/ppermute | solution.py:504
  14.7 5.1 %collective-permute-start.4 = (f32[13,16,128]{2,1,0:T(8,128)S(1)}, f32[13,16,128]{2,1,0:T(8,128)S(1)}, u32[]{:S(2)}, u32[]{:S(2)}) collective-permute-start(f32[13,16,128]{2,1,0:T(8,128)S(1)} %param.6), channel_id=1, source_target_pairs={{0,8},{4,12},{8,0},{12,4},{16,24},{20,28},{24,16},{28,20},{32,40},... | collective-permute-start | bytes 319496 | tf_op jit(solution)/shard_map/cond/branch_2_fun/ppermute | solution.py:504
  20.0 0.7 copy-start
  20.7 1.0 %copy-start.1 = (f32[2,1,8,3,16,128]{5,4,3,2,1,0:T(8,128)S(1)}, f32[2,1,8,3,16,128]{5,4,3,2,1,0:T(8,128)}, u32[]{:S(2)}) copy-start(f32[2,1,8,3,16,128]{5,4,3,2,1,0:T(8,128)} %param.32) | copy-start | bytes 1179652
  21.7 0.7 copy-start.2
  22.4 0.7 copy-start.3
  23.1 0.7 copy-start.4
  23.7 1.0 %copy-start.5 = (bf16[768,256]{1,0:T(8,128)(2,1)S(1)}, bf16[768,256]{1,0:T(8,128)(2,1)}, u32[]{:S(2)}) copy-start(bf16[768,256]{1,0:T(8,128)(2,1)} %constant.53.clone.ztab) | copy-start | bytes 1179652
  24.7 1.0 %copy-start.6 = (bf16[256,768]{1,0:T(8,128)(2,1)S(1)}, bf16[256,768]{1,0:T(8,128)(2,1)}, u32[]{:S(2)}) copy-start(bf16[256,768]{1,0:T(8,128)(2,1)} %constant.52.clone.ytab) | copy-start | bytes 1179652
  25.7 0.7 copy-start.7
where the time goes:
time: 96.8 us; the launch traced here: 95.7 us
  Pallas kernels  67.1 us (69%)
  waiting for transfers between devices  9.54 us (10%)
  local copies, waits for them, and re-layouts  9.24 us (10%)
  starting transfers between devices  5.99 us (6%)
  between operations  2.69 us (3%)
    pallas_call x1, Pallas kernels, kernel_call(): pl.pallas_call(functools.partial(kernel, float(kpoints), row_g), out_shap...  67.1 us
    ppermute x2, waiting for transfers between devices, along(): return lambda block: lax.ppermute(block, 'ka', pairs)  9.54 us
    unnamed x17, local copies, waits for them, and re-layouts  8.57 us
    ppermute x2, starting transfers between devices, along(): return lambda block: lax.ppermute(block, 'ka', pairs)  5.99 us
  transfers between devices with their start and end apart: 2, of which 2 were waited for; matrix products, arithmetic and copies ran while one was open for 0% of the time, Pallas kernels for 0%

commit v1 on v0

--- a/solution.py
+++ b/solution.py
@@ -16,21 +16,18 @@
 SIDE = 4
 CUT = 384
 EXTRA = 128
+WIDE = 768
+FIRST = 0
 ORDER = (
-    "S0", "C00", "C01", "C02", "rs1_0", "C03", "S1", "C10", "C11", "fin_0", "Hs00", "Hs01", "Is000",
-    "Is010", "C12", "rs1_1", "C13", "Itm000", "Itp000", "Itm010", "Itp010", "Htm00", "Htp00",
-    "Is001", "Is002", "Htm01", "Htp01", "Is011", "Is012", "Os000", "Os010", "fin_1", "Hs10", "Hs11",
-    "Is100", "Is110", "Itm001", "Itp001", "Itm002", "Itp002", "Is003", "Itm011", "Itp011", "Itm012",
-    "Itp012", "Is013", "Otm010", "Otp010", "Itm100", "Itp100", "Htm10", "Htp10", "Is101", "Is102",
-    "Otm000", "Otp000", "Os001", "Os002", "Itm110", "Itp110", "Os011", "Itm003", "Itp003", "Htm11",
-    "Htp11", "Is111", "Is112", "Os012", "Itp013", "Itm013", "Os100", "R00", "Is103", "Itm101",
-    "Itp101", "Itm102", "Itp102", "Is113", "Otm001", "Otp001", "Otm011", "Otp011", "Os003", "M00",
-    "Itm111", "Itp111", "Itm112", "Itp112", "Otm002", "Otp002", "Os110", "Os013", "Otm012",
-    "Otp012", "Itm103", "Itp103", "Os101", "Os102", "Otp100", "Otm100", "Itp113", "Itm113", "R01",
-    "Otm110", "Otp110", "Otp003", "Otm003", "Os111", "Os112", "Otm013", "Otp013", "M01", "Os103",
-    "R02", "Otp101", "Otm101", "Otp102", "Otm102", "Otm111", "Otp111", "R10", "Os113", "M02",
-    "Otm112", "Otp112", "R03", "Otp103", "Otm103", "M10", "Otm113", "Otp113", "R11", "M03", "R12",
-    "R13", "M11", "M12", "M13",
+    0, 1, 5, 9, 2, 6, 4, 10, 8, 3, 12, 7, 11, 13, 89, 90, 94, 98, 14, 15, 48, 18, 51, 21, 54, 91,
+    93, 95, 97, 99, 101, 92, 96, 100, 102, 53, 20, 19, 52, 22, 23, 55, 56, 34, 17, 16, 27, 50, 49,
+    60, 67, 24, 57, 103, 104, 137, 107, 140, 110, 143, 25, 58, 41, 36, 35, 37, 62, 61, 63, 29, 28,
+    30, 69, 68, 70, 74, 26, 59, 145, 142, 141, 109, 108, 144, 112, 111, 106, 105, 116, 123, 43, 139,
+    138, 149, 156, 42, 44, 38, 39, 64, 65, 32, 76, 31, 71, 130, 75, 77, 72, 81, 146, 163, 113, 114,
+    147, 150, 152, 151, 119, 118, 117, 157, 159, 158, 124, 126, 125, 45, 46, 66, 82, 40, 73, 132,
+    33, 165, 115, 131, 133, 148, 78, 164, 166, 79, 153, 47, 121, 160, 154, 128, 120, 85, 83, 161,
+    127, 134, 170, 80, 135, 167, 168, 86, 122, 155, 84, 129, 162, 136, 171, 169, 87, 172, 174, 176,
+    88, 173, 175, 177,
 )
 
 
@@ -51,10 +48,9 @@
     return np.block([[cos, -sin], [sin, cos]]).astype(np.float32)
 
 
-def x_table(extent, norm):
-    index = np.arange(extent)
-    angle = 2 * np.pi * (np.outer(index, index) % extent) / extent
-    return (np.concatenate([np.cos(angle), np.sin(angle)], 1) * norm).astype(np.float32)
+def x_phases(extent, planes, norm):
+    angle = 2 * np.pi * (np.outer(np.arange(planes), np.arange(extent)) % extent) / extent
+    return np.cos(angle) * norm, np.sin(angle) * norm
 
 
 def split_rows(value):
@@ -62,17 +58,31 @@
     return high, (value - high.astype(f32)).astype(bf16)
 
 
+def thrice(table, axis):
+    high, low = jnp.split(table, 2, axis)
+    return jnp.concatenate([high, high, low], axis)
+
+
 def split_table(table, axis):
     high = table.astype(jnp.bfloat16)
     low = (table - high.astype(np.float32)).astype(jnp.bfloat16)
-    return jnp.asarray(np.concatenate([high, high, low], axis))
+    return jnp.asarray(np.concatenate([high, low], axis))
 
 
 def kernel(
-    kpoints, row_g, shift, xtab, freq, cond_e, packed, cond, gvec, ytab, ztab, out,
+    kpoints, row_g, norm, packed, shift_in, freq_in, cond_e_in, gvec_in, cond_in, ytab_in, ztab_in, out,
     g00, g01, g10, g11, part, r1, s2, r2, spec, phase, wtile, rt, left, sel, wsel,
+    shift, freq, cond_e, cond, gvec, ytab, ztab, loads,
     send, recv, rsend, rrecv,
 ):
+    inputs = (shift_in, freq_in, cond_e_in, gvec_in, cond_in, ytab_in, ztab_in)
+    held_here = (shift, freq, cond_e, gvec, cond, ytab, ztab)
+    fetches = [
+        pltpu.make_async_copy(there, here, loads.at[i])
+        for i, (there, here) in enumerate(zip(inputs, held_here))
+    ]
+    for fetch in fetches:
+        fetch.start()
     ka = lax.axis_index("ka")
     slab = lax.axis_index("slab")
     zlo, core = slab // 2, slab % 2
@@ -83,7 +93,7 @@
     xi, hi, yi = coords
     bands, planes, ny, nz = cond.shape[1:]
     nv = 2
-    nx = xtab.shape[0]
+    nx = planes * 4
     rows = bands * ny
     height = planes * 2 * bands
     fields = nv * 2 * planes
@@ -121,6 +131,9 @@
             if name not in waited:
                 waited.add(name)
                 copies[name].wait_recv()
+
+    for fetch in fetches:
+        fetch.wait()
 
     q = shift[0]
     folds = [
@@ -179,13 +192,13 @@
             im = (vr * ci - vi * cr).reshape(rows, nz)
             columns.append(jnp.concatenate([re, im], 0))
         high, low = split_rows(jnp.concatenate(columns, 1))
-        t = jnp.dot(ytab[...], jnp.concatenate([high, low, high], 0), preferred_element_type=f32)
+        t = jnp.dot(thrice(ytab[...], 1), jnp.concatenate([high, low, high], 0), preferred_element_type=f32)
         t = [
             jnp.concatenate([t[:rows, x * nz : (x + 1) * nz], t[rows:, x * nz : (x + 1) * nz]], 1)
             for x in range(planes)
         ]
         high, low = split_rows(jnp.concatenate(t, 0))
-        f = jnp.dot(jnp.concatenate([high, low, high], 1), ztab[...], preferred_element_type=f32)
+        f = jnp.dot(jnp.concatenate([high, low, high], 1), thrice(ztab[...], 0), preferred_element_type=f32)
         for x in range(planes):
             fx = f[x * rows : (x + 1) * rows]
             both = [fx[:, :nz].reshape(ny, bands, nz), fx[:, nz:].reshape(ny, bands, nz)]
@@ -196,7 +209,7 @@
                 spec[:, here, odd * nz : (odd + 1) * nz] = high
                 spec[:, here, (2 + odd) * nz : (3 + odd) * nz] = low
 
-    def columns_of(v, j):
+    def columns_of(v, j, tile=None):
         def step(i, _):
             cols = pl.ds(pl.multiple_of(targets[j] * block_g + i * TILE, TILE), TILE)
             local = pl.ds(pl.multiple_of(i * TILE, TILE), TILE)
@@ -206,14 +219,18 @@
             if v == 0:
                 gx = g // (nz * ny) - folds[0]
                 gx = jnp.where(gx < 0, gx + nx, gx)
-                cosines = [jnp.zeros((1, TILE), f32) for _ in range(planes)]
-                sines = list(cosines)
-                for m in range(nx):
-                    same = gx == m
-                    for x in range(planes):
-                        plane = slab * planes + x
-                        cosines[x] = jnp.where(same, xtab[plane, m], cosines[x])
-                        sines[x] = jnp.where(same, xtab[plane, nx + m], sines[x])
+                turn = (slab * gx) % 4
+                flip = turn % 2 == 1
+                sign = jnp.where(turn >= 2, -1.0, 1.0)
+                cos_of, sin_of = x_phases(nx, planes, norm)
+                cosines, sines = [], []
+                for x in range(planes):
+                    c, s = jnp.full((1, TILE), norm, f32), jnp.zeros((1, TILE), f32)
+                    for m in range(1, nx if x else 1):
+                        c = jnp.where(gx == m, float(cos_of[x, m]), c)
+                        s = jnp.where(gx == m, float(sin_of[x, m]), s)
+                    cosines.append(sign * jnp.where(flip, -s, c))
+                    sines.append(sign * jnp.where(flip, c, s))
                 for x in range(planes):
                     phase[x : x + 1, cols] = cosines[x]
                     phase[planes + x : planes + x + 1, cols] = sines[x]
@@ -238,42 +255,44 @@
             part[v, j, :, local] = jnp.concatenate([re, im], 0)
             return 0
 
-        lax.fori_loop(0, block_g // TILE, step, 0)
+        if tile is not None:
+            step(tile, 0)
+        else:
+            lax.fori_loop(0, block_g // TILE, step, 0)
 
     actions = {}
 
     def add(name, call):
         actions[name] = call
 
-    def first_columns():
-        columns_of(0, 0)
-        pl.semaphore_wait(barrier, len(friends))
-        start("ra0", part.at[0, 0], r1.at[0, 0], partner)
-
-    def compute(v, j):
-        if (v, j) == (0, 0):
-            return first_columns
-        if j % 2:
-            return lambda: columns_of(v, j)
-
+    def tile_cols(i):
+        return pl.ds(i * TILE, TILE)
+
+    def compute(v, j, i):
         def call():
-            columns_of(v, j)
-            name = ("ra", None, "rb")[j] + str(v)
-            start(name, part.at[v, j], r1.at[v, j // 2], partner)
+            columns_of(v, j, i)
+            if (v, j, i) == (0, 0, 0):
+                pl.semaphore_wait(barrier, len(friends))
+            if j == 0:
+                here = part.at[v, 0, :, tile_cols(i)]
+                start(f"ra{v}{i}", here, r1.at[v, 0, :, tile_cols(i)], partner)
+            if j == 2 and i == block_g // TILE - 1:
+                start(f"rb{v}", part.at[v, 2], r1.at[v, 1], partner)
 
         return call
 
-    def across_sum(v):
+    def across_sum(v, i):
         def call():
-            need(f"ra{v}")
-            s2[v] = part[v, 1] + r1[v, 0]
-            start(f"r2{v}", s2.at[v], r2.at[v], across)
+            need(f"ra{v}{i}")
+            cols = tile_cols(i)
+            s2[v, :, cols] = part[v, 1, :, cols] + r1[v, 0, :, cols]
+            start(f"r2{v}{i}", s2.at[v, :, cols], r2.at[v, :, cols], across)
 
         return call
 
     def finish_block(v):
         def call():
-            need(f"rb{v}", f"r2{v}")
+            need(f"rb{v}", *[f"r2{v}{i}" for i in range(block_g // TILE)])
             total = (part[v, 3] + r1[v, 1] + r2[v]).astype(bf16)
             bufs[v][0][0, 0, 0] = total[:, :half_g]
             if v == 0:
@@ -321,6 +340,45 @@
     def high_blocks(ref):
         return ref.at[pl.ds(2, 2)]
 
+    def units_of(h):
+        if h == 0:
+            return {"0": (0, 1), "1": (1, 1), "2": (2, 1), "3": (3, 1)}
+        return {"a": (0, 2), "b": (2, 2)}
+
+    def fine(v, side, h, axis):
+        g = bufs[v][side]
+        k = f"{v}{side}{h}"
+        ready = ((), (f"I{k}1p",), (f"I{k}1m",), (f"I{k}2p", f"I{k}2m"))
+        units = units_of(h)
+
+        def begin(unit, first, count):
+            def call():
+                for i in range(first, first + count):
+                    need(*ready[i])
+                blocks = pl.ds(first, count)
+                for way, slot, move in (("p", 1, 1), ("m", 2, 3)):
+                    start(
+                        f"O{k}{way}{unit}", g.at[h, 0, blocks], g.at[h, slot, blocks],
+                        neighbour(axis, move),
+                    )
+
+            return call
+
+        def turn(way, first, slot, move):
+            def call():
+                for unit, (at, count) in units.items():
+                    if first <= at < first + 2:
+                        need(f"O{k}{way}{unit}")
+                blocks = pl.ds(first, 2)
+                start(f"O{k}2{way}", g.at[h, slot, blocks], g.at[h, 3, blocks], neighbour(axis, move))
+
+            return call
+
+        for unit, (first, count) in units.items():
+            add(f"Os{unit}{k}", begin(unit, first, count))
+        add(f"Otp{k}", turn("p", 0, 1, 1))
+        add(f"Otm{k}", turn("m", 2, 2, 3))
+
     row_copies = {}
 
     def natural(v, side, h, cols):
@@ -335,7 +393,10 @@
         chunk = v * SIDE + h
 
         def call():
-            need(*[f"O{v}{side}{h}2{way}" for side in range(2) for way in "pm"])
+            for side in range(2):
+                for way in "pm":
+                    need(f"O{v}{side}{h}2{way}", *[f"O{v}{side}{h}{way}{u}" for u in units_of(h)])
+                    need(f"O01{h}2{way}", *[f"O01{h}{way}{u}" for u in units_of(h)])
             held = [
                 pltpu.make_async_remote_copy(
                     src_ref=rt.at[chunk], dst_ref=rt.at[chunk], send_sem=rsend.at[chunk, d],
@@ -383,24 +444,27 @@
             for side in range(2):
 
                 def column(i, _, side=side):
-                    cols = pl.ds(pl.multiple_of(i * 256, 256), 256)
-                    there = pl.ds(pl.multiple_of(side * half_g + i * 256, 256), 256)
+                    cols = pl.ds(pl.multiple_of(i * WIDE, WIDE), WIDE)
+                    there = pl.ds(pl.multiple_of(side * half_g + i * WIDE, WIDE), WIDE)
                     product = jnp.dot(left[...], natural(v, side, h, cols), preferred_element_type=f32)
-                    if chunk == 0:
+                    if chunk == FIRST:
                         out[:, there] = product
                     else:
                         out[:, there] += product
                     return 0
 
-                lax.fori_loop(0, half_g // 256, column, 0)
+                lax.fori_loop(0, half_g // WIDE, column, 0)
 
         return call
 
     for v in range(nv):
         add(f"S{v}", lambda v=v: spectrum(v))
-        for j in range(4):
-            add(f"C{v}{j}", compute(v, j))
-        add(f"rs1_{v}", across_sum(v))
+        tiles = block_g // TILE
+        for i in range(tiles):
+            for j in range(3):
+                add(f"T{v}{j}{i}", compute(v, j, i))
+            add(f"rs{v}{i}", across_sum(v, i))
+        add(f"C{v}3", lambda v=v: columns_of(v, 3))
         add(f"fin_{v}", finish_block(v))
         for side in range(2):
             g = bufs[v][side]
@@ -411,19 +475,18 @@
             for h in range(SIDE):
                 ring(f"I{k}{h}1", f"I{k}{h}2", (f"Is{k}{h}", f"Itp{k}{h}", f"Itm{k}{h}"), inner,
                      lambda j, g=g, h=h: g.at[h, 0, j], low_lanes, high_lanes)
-                ring(f"O{k}{h}1", f"O{k}{h}2", (f"Os{k}{h}", f"Otp{k}{h}", f"Otm{k}{h}"), outer,
-                     lambda j, g=g, h=h: g.at[h, j], low_blocks, high_blocks)
+                fine(v, side, h, outer)
                 before = ((), (f"H{k}1p",), (f"H{k}1m",), (f"H{k}2p", f"H{k}2m"))[h]
                 after(before, f"Is{k}{h}")
-                after([f"I{k}{h}{n}{way}" for n in "12" for way in "pm"], f"Os{k}{h}")
         for h in range(SIDE):
             add(f"R{v}{h}", ship_rows(v, h))
             add(f"M{v}{h}", multiply(v, h))
 
     weights()
-    for name in ORDER:
-        actions.pop(name)()
-    assert not actions
+    steps = list(actions.values())
+    assert sorted(ORDER) == list(range(len(steps)))
+    for at in ORDER:
+        steps[at]()
 
     for c in copies.values():
         c.wait_send()
@@ -437,18 +500,19 @@
 
 def kernel_call(shift, freq, cond_e, packed, cond, gvec, norm, slabs, kpoints):
     bands, planes, ny, nz = cond.shape[1:]
+    ytab, ztab = split_table(y_table(bands, ny), 1), split_table(z_table(nz), 0)
+    fetched = (shift, freq, cond_e, gvec, cond, ytab, ztab)
     total = gvec.shape[1]
-    nx = planes * slabs
     block_g, row_g, freqs = total // slabs, total // kpoints, freq.shape[0]
     half = 2 * bands
     tall = (row_g + 3 * freqs + 15) // 16 * 16
     vm = pl.BlockSpec(memory_space=pltpu.VMEM)
-    sm = pl.BlockSpec(memory_space=pltpu.SMEM)
-    count = 3 * 2 + 4 * (4 + 16 + 16)
+    far = pl.BlockSpec(memory_space=pltpu.HBM)
+    count = 2 * (3 + 1 + 3) + 4 * (4 + 16 + 10 + 3 * 6)
     return pl.pallas_call(
-        functools.partial(kernel, float(kpoints), row_g),
+        functools.partial(kernel, float(kpoints), row_g, norm),
         out_shape=jax.ShapeDtypeStruct((freqs * 2 * row_g, block_g), f32),
-        in_specs=[sm] * 4 + [vm] * 5,
+        in_specs=[vm] + [far] * 7,
         out_specs=vm,
         scratch_shapes=[
             pltpu.VMEM((4, 4, 4, half, block_g // 2), bf16),
@@ -466,26 +530,26 @@
             pltpu.VMEM((freqs * 2 * row_g, 256), bf16),
             pltpu.VMEM((row_g, block_g // 2), bf16),
             pltpu.VMEM((2, tall - row_g, EXTRA), bf16),
+            pltpu.SMEM(shift.shape, jnp.int32),
+            pltpu.SMEM(freq.shape, f32),
+            pltpu.SMEM(cond_e.shape, f32),
+            pltpu.VMEM(cond.shape, f32),
+            pltpu.VMEM(gvec.shape, jnp.int32),
+            pltpu.VMEM(ytab.shape, bf16),
+            pltpu.VMEM(ztab.shape, bf16),
+            pltpu.SemaphoreType.DMA((7,)),
             pltpu.SemaphoreType.DMA((count,)),
             pltpu.SemaphoreType.DMA((count,)),
             pltpu.SemaphoreType.DMA((8, 3)),
             pltpu.SemaphoreType.DMA((8,)),
         ],
         compiler_params=pltpu.CompilerParams(
-            collective_id=0, has_side_effects=True, vmem_limit_bytes=48 * 1024 * 1024
+            collective_id=0, has_side_effects=True, vmem_limit_bytes=46_000_000
         ),
         cost_estimate=pl.CostEstimate(flops=10**10, bytes_accessed=10**7, transcendentals=0),
         name="response",
     )(
-        shift,
-        jnp.asarray(x_table(nx, norm)),
-        freq,
-        cond_e,
-        packed,
-        cond,
-        gvec,
-        split_table(y_table(bands, ny), 1),
-        split_table(z_table(nz), 0),
+        packed, *[pltpu.with_memory_space_constraint(a, pltpu.HBM) for a in fetched],
     )
 
 

time: 96.8 us -> 86.5 us (0.89)
  Pallas kernels: 67.1 us -> 60.7 us
  local copies, waits for them, and re-layouts: 9.24 us -> 2.86 us
  waiting for transfers between devices: 9.54 us -> 10.8 us
    pallas_call x1, Pallas kernels: 67.1 us -> 60.7 us  [kernel_call(): pl.pallas_call(functools.partial(kernel, float(kpoints), row_g, norm), ou...]
    unnamed x17 -> x1, local copies, waits for them, and re-layouts: 8.57 us -> 2.19 us
    ppermute x2, waiting for transfers between devices: 9.54 us -> 10.8 us  [along(): return lambda block: lax.ppermute(block, 'ka', pairs)]
where the time goes in v1:
time: 86.5 us; the launch traced here: 85 us
  Pallas kernels  60.7 us (70%)
  waiting for transfers between devices  10.8 us (12%)
  starting transfers between devices  6.91 us (8%)
  local copies, waits for them, and re-layouts  2.86 us (3%)
  between operations  2.67 us (3%)
  other arithmetic  0.9 us (1%)
    pallas_call x1, Pallas kernels, kernel_call(): pl.pallas_call(functools.partial(kernel, float(kpoints), row_g, norm), ou...  60.7 us
    ppermute x2, waiting for transfers between devices, along(): return lambda block: lax.ppermute(block, 'ka', pairs)  10.8 us
    ppermute x2, starting transfers between devices, along(): return lambda block: lax.ppermute(block, 'ka', pairs)  6.91 us
    unnamed x1, local copies, waits for them, and re-layouts  2.19 us
  transfers between devices with their start and end apart: 2, of which 2 were waited for; matrix products, arithmetic and copies ran while one was open for 0% of the time, Pallas kernels for 0%

profile of v1, /device:TPU:33, one launch (start us, length us, event | category | flops | bytes accessed | tf_op | source)
XLA Modules:
  0.0 85.0 jit_solution(14145718499656670761)
XLA Ops:
  2.6 0.7 pad_bitcast_fusion
  3.3 0.9 %pad_maximum_fusion = f32[13,16,128]{2,1,0:T(8,128)S(1)} fusion(f32[1,16,128]{2,1,0:T(8,128)S(1)} %pad_bitcast_fusion, f32[12,16,128]{2,1,0:T(8,128)} %bitcast.9), kind=kLoop, calls=%fused_computation | loop fusion | flops 26624 | bytes 212992 | tf_op jit(solution)/shard_map/concatenate | solution.py:587
  4.2 10.4 %conditional.2 = (f32[13,16,128]{2,1,0:T(8,128)S(1)}) conditional(s32[]{:T(128)} %clamp.7, f32[13,16,128]{2,1,0:T(8,128)S(1)} %pad_maximum_fusion, f32[13,16,128]{2,1,0:T(8,128)S(1)} %pad_maximum_fusion, f32[13,16,128]{2,1,0:T(8,128)S(1)} %pad_maximum_fusion, f32[13,16,128]{2,1,0:T(8,128)S(1)} %pad_maximum_fusion), branch_computations={%region_0.1_spmd, %region_1.2_spmd, %region_2.3_spmd, %region_3.4_... | conditional | bytes 639024 | solution.py:573
  4.2 3.0 %collective-permute-start = (f32[13,16,128]{2,1,0:T(8,128)S(1)}, f32[13,16,128]{2,1,0:T(8,128)S(1)}, u32[]{:S(2)}, u32[]{:S(2)}) collective-permute-start(f32[13,16,128]{2,1,0:T(8,128)S(1)} %param.1), channel_id=1, source_target_pairs={{0,16},{4,20},{8,24},{12,28},{16,32},{20,36},{24,40},{28,44},{32,4... | collective-permute-start | bytes 319496 | tf_op jit(solution)/shard_map/cond/branch_1_fun/ppermute | solution.py:568
  7.2 7.4 %collective-permute-done = f32[13,16,128]{2,1,0:T(8,128)S(1)} collective-permute-done((f32[13,16,128]{2,1,0:T(8,128)S(1)}, f32[13,16,128]{2,1,0:T(8,128)S(1)}, u32[]{:S(2)}, u32[]{:S(2)}) %collective-permute-start) | collective-permute-done | bytes 106528 | tf_op jit(solution)/shard_map/cond/branch_1_fun/ppermute | solution.py:568
  14.6 7.5 %conditional.3 = (f32[13,16,128]{2,1,0:T(8,128)S(1)}) conditional(s32[]{:T(128)} %clamp.6, f32[13,16,128]{2,1,0:T(8,128)S(1)} %get-tuple-element.47, f32[13,16,128]{2,1,0:T(8,128)S(1)} %get-tuple-element.47, f32[13,16,128]{2,1,0:T(8,128)S(1)} %get-tuple-element.47, f32[13,16,128]{2,1,0:T(8,128)S(1)} %get-tuple-element.47, ...), branch_computations={%region_4.5_spmd, %region_5.6_spmd, %region_6.7_spmd, %region_7.8_... | conditional | bytes 639024 | solution.py:574
  14.7 3.9 %collective-permute-start.8 = (f32[13,16,128]{2,1,0:T(8,128)S(1)}, f32[13,16,128]{2,1,0:T(8,128)S(1)}, u32[]{:S(2)}, u32[]{:S(2)}) collective-permute-start(f32[13,16,128]{2,1,0:T(8,128)S(1)} %param.10), channel_id=1, source_target_pairs={{0,72},{4,76},{8,64},{12,68},{16,88},{20,92},{24,80},{28,84},{32,1... | collective-permute-start | bytes 319496 | tf_op jit(solution)/shard_map/cond/branch_6_fun/ppermute | solution.py:568
  18.6 3.4 %collective-permute-done.8 = f32[13,16,128]{2,1,0:T(8,128)S(1)} collective-permute-done((f32[13,16,128]{2,1,0:T(8,128)S(1)}, f32[13,16,128]{2,1,0:T(8,128)S(1)}, u32[]{:S(2)}, u32[]{:S(2)}) %collective-permute-start.8) | collective-permute-done | bytes 106528 | tf_op jit(solution)/shard_map/cond/branch_6_fun/ppermute | solution.py:568
  22.1 60.7 %response.1 = f32[768,1536]{1,0:T(8,128)S(1)} custom-call(f32[13,16,128]{2,1,0:T(8,128)S(1)} %get-tuple-element.48.packed, s32[64]{0:T(128)} %shift_in.1, f32[4]{0:T(128)} %freq_in.1, f32[1,8]{1,0:T(1,128)} %cond_e_in.1, s32[1,6144]{1,0:T(1,128)} %bitcast.15, f32[2,8,3,16,128]{4,3,2,1,0:T(8,128)} %bitcast.14, bf16[256,512]{1,0:T(8,128)(2,1)} %constant.49.clone.ytab_in, ...), custom_call_target="tpu_custom_call" | custom-call | flops 10000000000 | bytes 10000000 | tf_op jit(solution)/shard_map/response/pallas_call | solution.py:512
  82.9 2.2 %copy.31 = f32[4,2,96,1536]{3,2,1,0:T(8,128)} copy(f32[4,2,96,1536]{3,2,1,0:T(8,128)S(1)} %bitcast.8) | data formatting | bytes 9437184
  (2 shorter events, 0.0 us)
Async XLA Ops:
  4.2 10.4 %collective-permute-start = (f32[13,16,128]{2,1,0:T(8,128)S(1)}, f32[13,16,128]{2,1,0:T(8,128)S(1)}, u32[]{:S(2)}, u32[]{:S(2)}) collective-permute-start(f32[13,16,128]{2,1,0:T(8,128)S(1)} %param.1), channel_id=1, source_target_pairs={{0,16},{4,20},{8,24},{12,28},{16,32},{20,36},{24,40},{28,44},{32,4... | collective-permute-start | bytes 319496 | tf_op jit(solution)/shard_map/cond/branch_1_fun/ppermute | solution.py:568
  14.7 7.3 %collective-permute-start.8 = (f32[13,16,128]{2,1,0:T(8,128)S(1)}, f32[13,16,128]{2,1,0:T(8,128)S(1)}, u32[]{:S(2)}, u32[]{:S(2)}) collective-permute-start(f32[13,16,128]{2,1,0:T(8,128)S(1)} %param.10), channel_id=1, source_target_pairs={{0,72},{4,76},{8,64},{12,68},{16,88},{20,92},{24,80},{28,84},{32,1... | collective-permute-start | bytes 319496 | tf_op jit(solution)/shard_map/cond/branch_6_fun/ppermute | solution.py:568

commit v2 on v1

--- a/solution.py
+++ b/solution.py
@@ -12,22 +12,21 @@
 HIGH = lax.Precision.HIGHEST
 MESH = pl.DeviceIdType.MESH
 f32, bf16 = jnp.float32, jnp.bfloat16
-TILE = 512
+TILE = 768
 SIDE = 4
 CUT = 384
 EXTRA = 128
 WIDE = 768
 FIRST = 0
 ORDER = (
-    0, 1, 5, 9, 2, 6, 4, 10, 8, 3, 12, 7, 11, 13, 89, 90, 94, 98, 14, 15, 48, 18, 51, 21, 54, 91,
-    93, 95, 97, 99, 101, 92, 96, 100, 102, 53, 20, 19, 52, 22, 23, 55, 56, 34, 17, 16, 27, 50, 49,
-    60, 67, 24, 57, 103, 104, 137, 107, 140, 110, 143, 25, 58, 41, 36, 35, 37, 62, 61, 63, 29, 28,
-    30, 69, 68, 70, 74, 26, 59, 145, 142, 141, 109, 108, 144, 112, 111, 106, 105, 116, 123, 43, 139,
-    138, 149, 156, 42, 44, 38, 39, 64, 65, 32, 76, 31, 71, 130, 75, 77, 72, 81, 146, 163, 113, 114,
-    147, 150, 152, 151, 119, 118, 117, 157, 159, 158, 124, 126, 125, 45, 46, 66, 82, 40, 73, 132,
-    33, 165, 115, 131, 133, 148, 78, 164, 166, 79, 153, 47, 121, 160, 154, 128, 120, 85, 83, 161,
-    127, 134, 170, 80, 135, 167, 168, 86, 122, 155, 84, 129, 162, 136, 171, 169, 87, 172, 174, 176,
-    88, 173, 175, 177,
+    0, 1, 5, 2, 6, 4, 3, 8, 7, 9, 85, 86, 90, 87, 10, 14, 89, 11, 44, 47, 50, 17, 91, 93, 88, 92,
+    94, 49, 15, 16, 48, 18, 19, 52, 51, 30, 13, 23, 12, 63, 46, 20, 53, 21, 45, 56, 95, 96, 99, 129,
+    132, 102, 135, 54, 31, 32, 33, 25, 26, 24, 65, 66, 64, 55, 22, 37, 58, 101, 100, 104, 103, 134,
+    137, 70, 57, 59, 98, 115, 133, 136, 97, 108, 34, 27, 131, 148, 130, 141, 35, 68, 28, 38, 39, 40,
+    67, 105, 77, 122, 106, 71, 73, 61, 60, 155, 138, 117, 72, 116, 118, 139, 110, 109, 36, 111, 78,
+    149, 150, 142, 29, 124, 151, 41, 144, 69, 143, 123, 125, 107, 157, 75, 62, 140, 42, 74, 156,
+    158, 119, 120, 112, 81, 113, 152, 153, 43, 79, 145, 146, 126, 127, 162, 76, 82, 121, 159, 80,
+    154, 160, 114, 147, 163, 128, 83, 161, 166, 164, 168, 84, 167, 165, 169,
 )
 
 
@@ -72,7 +71,7 @@
 def kernel(
     kpoints, row_g, norm, packed, shift_in, freq_in, cond_e_in, gvec_in, cond_in, ytab_in, ztab_in, out,
     g00, g01, g10, g11, part, r1, s2, r2, spec, phase, wtile, rt, left, sel, wsel,
-    shift, freq, cond_e, cond, gvec, ytab, ztab, loads,
+    shift, freq, cond_e, cond, gvec, ytab, ztab, counter, loads,
     send, recv, rsend, rrecv,
 ):
     inputs = (shift_in, freq_in, cond_e_in, gvec_in, cond_in, ytab_in, ztab_in)
@@ -214,13 +213,13 @@
             cols = pl.ds(pl.multiple_of(targets[j] * block_g + i * TILE, TILE), TILE)
             local = pl.ds(pl.multiple_of(i * TILE, TILE), TILE)
             g = gvec[:, cols]
-            gz = (g % nz - folds[2] + nz) % nz
-            gy = (g // nz % ny - folds[1] + ny) % ny
+            gz = (g - folds[2] + nz) & (nz - 1)
+            gy = ((g >> 7) - folds[1] + ny) & (ny - 1)
             if v == 0:
-                gx = g // (nz * ny) - folds[0]
+                gx = (g >> 11) - folds[0]
                 gx = jnp.where(gx < 0, gx + nx, gx)
-                turn = (slab * gx) % 4
-                flip = turn % 2 == 1
+                turn = (slab * gx) & 3
+                flip = (turn & 1) == 1
                 sign = jnp.where(turn >= 2, -1.0, 1.0)
                 cos_of, sin_of = x_phases(nx, planes, norm)
                 cosines, sines = [], []
@@ -237,12 +236,13 @@
             else:
                 cosines = [phase[x : x + 1, cols] for x in range(planes)]
                 sines = [phase[planes + x : planes + x + 1, cols] for x in range(planes)]
-            code = gz + gy % 2 * nz
-            hot = (lax.broadcasted_iota(jnp.int32, (2 * nz, TILE), 0) == code).astype(f32).astype(bf16)
+            code = gz + (gy & 1) * nz
+            same = counter[...] == jnp.broadcast_to(code.astype(f32).astype(bf16), counter.shape)
+            hot = jnp.where(same, jnp.ones(counter.shape, bf16), jnp.zeros(counter.shape, bf16))
             hot = jnp.concatenate([hot, hot], 0)
             table = spec[...].reshape(ny // 2 * height, 4 * nz)
             picked = jnp.dot(table, hot, preferred_element_type=f32)
-            which = jnp.broadcast_to(gy // 2, (height, TILE))
+            which = jnp.broadcast_to(gy >> 1, (height, TILE))
             acc = picked[:height]
             for k in range(1, ny // 2):
                 acc = jnp.where(which == k, picked[k * height : (k + 1) * height], acc)
@@ -482,6 +482,7 @@
             add(f"R{v}{h}", ship_rows(v, h))
             add(f"M{v}{h}", multiply(v, h))
 
+    counter[...] = lax.broadcasted_iota(jnp.int32, counter.shape, 0).astype(f32).astype(bf16)
     weights()
     steps = list(actions.values())
     assert sorted(ORDER) == list(range(len(steps)))
@@ -537,6 +538,7 @@
             pltpu.VMEM(gvec.shape, jnp.int32),
             pltpu.VMEM(ytab.shape, bf16),
             pltpu.VMEM(ztab.shape, bf16),
+            pltpu.VMEM((2 * nz, TILE), bf16),
             pltpu.SemaphoreType.DMA((7,)),
             pltpu.SemaphoreType.DMA((count,)),
             pltpu.SemaphoreType.DMA((count,)),

time: 86.5 us -> 85.1 us (0.984)
  waiting for transfers between devices: 10.8 us -> 6.75 us
  Pallas kernels: 60.7 us -> 62.9 us
    ppermute x2, waiting for transfers between devices: 10.8 us -> 6.75 us  [along(): return lambda block: lax.ppermute(block, 'ka', pairs)]
    pallas_call x1, Pallas kernels: 60.7 us -> 62.9 us  [kernel_call(): pl.pallas_call(functools.partial(kernel, float(kpoints), row_g, norm), ou...]
where the time goes in v2:
time: 85.1 us; the launch traced here: 84 us
  Pallas kernels  62.9 us (74%)
  starting transfers between devices  7.69 us (9%)
  waiting for transfers between devices  6.75 us (8%)
  local copies, waits for them, and re-layouts  2.86 us (3%)
  between operations  2.67 us (3%)
  other arithmetic  0.9 us (1%)
    pallas_call x1, Pallas kernels, kernel_call(): pl.pallas_call(functools.partial(kernel, float(kpoints), row_g, norm), ou...  62.9 us
    ppermute x2, starting transfers between devices, along(): return lambda block: lax.ppermute(block, 'ka', pairs)  7.69 us
    ppermute x2, waiting for transfers between devices, along(): return lambda block: lax.ppermute(block, 'ka', pairs)  6.75 us
    unnamed x1, local copies, waits for them, and re-layouts  2.19 us
  transfers between devices with their start and end apart: 2, of which 2 were waited for; matrix products, arithmetic and copies ran while one was open for 0% of the time, Pallas kernels for 0%

profile of v2, /device:TPU:33, one launch (start us, length us, event | category | flops | bytes accessed | tf_op | source)
XLA Modules:
  0.0 84.0 jit_solution(4562153061729000844)
XLA Ops:
  2.6 0.7 pad_bitcast_fusion
  3.3 0.9 %pad_maximum_fusion = f32[13,16,128]{2,1,0:T(8,128)S(1)} fusion(f32[1,16,128]{2,1,0:T(8,128)S(1)} %pad_bitcast_fusion, f32[12,16,128]{2,1,0:T(8,128)} %bitcast.9), kind=kLoop, calls=%fused_computation | loop fusion | flops 26624 | bytes 212992 | tf_op jit(solution)/shard_map/concatenate | solution.py:589
  4.2 8.9 %conditional.2 = (f32[13,16,128]{2,1,0:T(8,128)S(1)}) conditional(s32[]{:T(128)} %clamp.7, f32[13,16,128]{2,1,0:T(8,128)S(1)} %pad_maximum_fusion, f32[13,16,128]{2,1,0:T(8,128)S(1)} %pad_maximum_fusion, f32[13,16,128]{2,1,0:T(8,128)S(1)} %pad_maximum_fusion, f32[13,16,128]{2,1,0:T(8,128)S(1)} %pad_maximum_fusion), branch_computations={%region_0.1_spmd, %region_1.2_spmd, %region_2.3_spmd, %region_3.4_... | conditional | bytes 639024 | solution.py:575
  4.2 5.1 %collective-permute-start.2 = (f32[13,16,128]{2,1,0:T(8,128)S(1)}, f32[13,16,128]{2,1,0:T(8,128)S(1)}, u32[]{:S(2)}, u32[]{:S(2)}) collective-permute-start(f32[13,16,128]{2,1,0:T(8,128)S(1)} %param.3), channel_id=1, source_target_pairs={{0,48},{4,52},{8,56},{12,60},{16,0},{20,4},{24,8},{28,12},{32,16},... | collective-permute-start | bytes 319496 | tf_op jit(solution)/shard_map/cond/branch_3_fun/ppermute | solution.py:570
  9.3 3.7 %collective-permute-done.2 = f32[13,16,128]{2,1,0:T(8,128)S(1)} collective-permute-done((f32[13,16,128]{2,1,0:T(8,128)S(1)}, f32[13,16,128]{2,1,0:T(8,128)S(1)}, u32[]{:S(2)}, u32[]{:S(2)}) %collective-permute-start.2) | collective-permute-done | bytes 106528 | tf_op jit(solution)/shard_map/cond/branch_3_fun/ppermute | solution.py:570
  13.1 5.8 %conditional.3 = (f32[13,16,128]{2,1,0:T(8,128)S(1)}) conditional(s32[]{:T(128)} %clamp.6, f32[13,16,128]{2,1,0:T(8,128)S(1)} %get-tuple-element.47, f32[13,16,128]{2,1,0:T(8,128)S(1)} %get-tuple-element.47, f32[13,16,128]{2,1,0:T(8,128)S(1)} %get-tuple-element.47, f32[13,16,128]{2,1,0:T(8,128)S(1)} %get-tuple-element.47, ...), branch_computations={%region_4.5_spmd, %region_5.6_spmd, %region_6.7_spmd, %region_7.8_... | conditional | bytes 639024 | solution.py:576
  13.1 2.6 %collective-permute-start.4 = (f32[13,16,128]{2,1,0:T(8,128)S(1)}, f32[13,16,128]{2,1,0:T(8,128)S(1)}, u32[]{:S(2)}, u32[]{:S(2)}) collective-permute-start(f32[13,16,128]{2,1,0:T(8,128)S(1)} %param.6), channel_id=1, source_target_pairs={{0,8},{4,12},{8,0},{12,4},{16,24},{20,28},{24,16},{28,20},{32,40},... | collective-permute-start | bytes 319496 | tf_op jit(solution)/shard_map/cond/branch_2_fun/ppermute | solution.py:570
  15.7 3.0 %collective-permute-done.4 = f32[13,16,128]{2,1,0:T(8,128)S(1)} collective-permute-done((f32[13,16,128]{2,1,0:T(8,128)S(1)}, f32[13,16,128]{2,1,0:T(8,128)S(1)}, u32[]{:S(2)}, u32[]{:S(2)}) %collective-permute-start.4) | collective-permute-done | bytes 106528 | tf_op jit(solution)/shard_map/cond/branch_2_fun/ppermute | solution.py:570
  18.9 62.9 %response.1 = f32[768,1536]{1,0:T(8,128)S(1)} custom-call(f32[13,16,128]{2,1,0:T(8,128)S(1)} %get-tuple-element.48.packed, s32[64]{0:T(128)} %shift_in.1, f32[4]{0:T(128)} %freq_in.1, f32[1,8]{1,0:T(1,128)} %cond_e_in.1, s32[1,6144]{1,0:T(1,128)} %bitcast.15, f32[2,8,3,16,128]{4,3,2,1,0:T(8,128)} %bitcast.14, bf16[256,512]{1,0:T(8,128)(2,1)} %constant.49.clone.ytab_in, ...), custom_call_target="tpu_custom_call" | custom-call | flops 10000000000 | bytes 10000000 | tf_op jit(solution)/shard_map/response/pallas_call | solution.py:513
  81.9 2.2 %copy.31 = f32[4,2,96,1536]{3,2,1,0:T(8,128)} copy(f32[4,2,96,1536]{3,2,1,0:T(8,128)S(1)} %bitcast.8) | data formatting | bytes 9437184
  (2 shorter events, 0.0 us)
Async XLA Ops:
  4.2 8.8 %collective-permute-start.2 = (f32[13,16,128]{2,1,0:T(8,128)S(1)}, f32[13,16,128]{2,1,0:T(8,128)S(1)}, u32[]{:S(2)}, u32[]{:S(2)}) collective-permute-start(f32[13,16,128]{2,1,0:T(8,128)S(1)} %param.3), channel_id=1, source_target_pairs={{0,48},{4,52},{8,56},{12,60},{16,0},{20,4},{24,8},{28,12},{32,16},... | collective-permute-start | bytes 319496 | tf_op jit(solution)/shard_map/cond/branch_3_fun/ppermute | solution.py:570
  13.1 5.6 %collective-permute-start.4 = (f32[13,16,128]{2,1,0:T(8,128)S(1)}, f32[13,16,128]{2,1,0:T(8,128)S(1)}, u32[]{:S(2)}, u32[]{:S(2)}) collective-permute-start(f32[13,16,128]{2,1,0:T(8,128)S(1)} %param.6), channel_id=1, source_target_pairs={{0,8},{4,12},{8,0},{12,4},{16,24},{20,28},{24,16},{28,20},{32,40},... | collective-permute-start | bytes 319496 | tf_op jit(solution)/shard_map/cond/branch_2_fun/ppermute | solution.py:570
